TPU v7x, 512 devices: a whole 4x4x16 slice. The times are simulated.
512 devices in a mesh: row: 16 (over y_hi, x, core), col: 32 (over z, y_lo).
Axes of the slice: x: 4, y: 4 (y_hi: 2, y_lo: 2; y = y_hi * 2 + y_lo), z: 16, core: 2. Of those that a mesh axis runs over, the one named last changes fastest.
Arguments:
- specimen: float32 [2, 2048, 8192], P(None, 'row', 'col'), may hold values from -6 to 6
- probe_field: float32 [2, 256, 256], replicated, may hold values from -6 to 6
- scan_offsets: int32 [16, 32, 2, 2], replicated, may hold values from -128 to 128, as said below
- live_counts: int32 [16, 32], replicated, may hold values from 1 to 2, as said below
- magnitudes: float32 [16, 32, 2, 256, 256], P('row', 'col'), may hold values from 0 to 2
Outputs:
- specimen_next: float32 [2, 2048, 8192], P(None, 'row', 'col')
- probe_next: float32 [2, 256, 256], replicated
Inputs may be any that keep to these rules, and one draw needn't show every extreme that they name: `scan_offsets`: rows of a patch start within -128 to 0 of the tile's first row, columns within -128 to 128 of its first column. Tile (a, b) owns the positions in its first live_counts[a, b] slots.
All inputs are finite; a program needn't handle non-finite values.
Results may differ from a plain program's by a relative error of at most 0.0003.
Values sent between devices are 32-bit elements; how exact they have to be, the bound alone decides.
A program may use at most 64 MiB of HBM per device.

v0:
```python
import math
import jax
import jax.numpy as jnp
from jax import lax
from jax.sharding import PartitionSpec as P

modulus_floor = 0.25
object_damping = 0.1
probe_damping = 0.1


def extended_2(block, sides, width):
    for axis, dim in sides:
        count = lax.axis_size(axis)
        forward = [(i, i + 1) for i in range(count - 1)]
        backward = [(target, source) for source, target in forward]
        low = lax.ppermute(
            lax.slice_in_dim(block, block.shape[dim] - width, None, axis=dim), axis, forward
        )
        high = lax.ppermute(lax.slice_in_dim(block, 0, width, axis=dim), axis, backward)
        block = jnp.concatenate([low, block, high], axis=dim)
    return block


def dft_tables(width):
    counter = jnp.arange(width, dtype=jnp.int32)
    phase = counter[:, None] * counter[None, :] % width
    angle = phase.astype(jnp.float32) * (2.0 * math.pi / width)
    factor = 1.0 / math.sqrt(width)
    return (jnp.cos(angle) * factor, jnp.sin(angle) * factor)


def matmul_right(left, table):
    return jnp.einsum("sjm,ml->sjl", left, table, precision=lax.Precision.HIGHEST)


def matmul_left(table, right):
    return jnp.einsum("kj,sjl->skl", table, right, precision=lax.Precision.HIGHEST)


def transform(wave_real, wave_imag, cosine, sine, direction):
    inner_real = matmul_right(wave_real, cosine) + direction * matmul_right(wave_imag, sine)
    inner_imag = matmul_right(wave_imag, cosine) - direction * matmul_right(wave_real, sine)
    outer_real = matmul_left(cosine, inner_real) + direction * matmul_left(sine, inner_imag)
    outer_imag = matmul_left(cosine, inner_imag) - direction * matmul_left(sine, inner_real)
    return (outer_real, outer_imag)


def fold_rims(wide, tile_r, tile_c, half):
    center = wide[:, 2 * half : 2 * half + tile_r, :]
    center = center.at[:, :half, :].add(wide[:, :half, :])
    center = center.at[:, tile_r - half :, :].add(wide[:, tile_r + 3 * half :, :])
    result = center[:, :, 2 * half : 2 * half + tile_c]
    result = result.at[:, :, :half].add(center[:, :, :half])
    result = result.at[:, :, tile_c - half :].add(center[:, :, tile_c + 3 * half :])
    return result


def shards(specimen, probe_field, scan_offsets, live_counts, magnitudes):
    width = probe_field.shape[1]
    half = width // 2
    tile_r = specimen.shape[1]
    tile_c = specimen.shape[2]
    slots = magnitudes.shape[2]
    row_place = lax.axis_index("row")
    col_place = lax.axis_index("col")
    zero_index = jnp.zeros((), jnp.int32)
    extended = extended_2(specimen, (("row", 1), ("col", 2)), half)
    offsets_here = scan_offsets[row_place, col_place]
    live = (jnp.arange(slots, dtype=jnp.int32) < live_counts[row_place, col_place]).astype(
        jnp.float32
    )[:, None, None]
    row_starts = offsets_here[:, 0] + half
    col_starts = offsets_here[:, 1] + half

    def extract(row_start, col_start):
        return lax.dynamic_slice(extended, (zero_index, row_start, col_start), (2, width, width))

    patches = jax.vmap(extract)(row_starts, col_starts)
    patch_real = patches[:, 0]
    patch_imag = patches[:, 1]
    probe_real = probe_field[0]
    probe_imag = probe_field[1]
    power = probe_real * probe_real + probe_imag * probe_imag
    cosine, sine = dft_tables(width)
    wave_real = probe_real * patch_real - probe_imag * patch_imag
    wave_imag = probe_real * patch_imag + probe_imag * patch_real
    far_real, far_imag = transform(wave_real, wave_imag, cosine, sine, 1.0)
    modulus = jnp.sqrt(far_real * far_real + far_imag * far_imag)
    factor = magnitudes[0, 0] / jnp.maximum(modulus, modulus_floor) - 1.0
    diff_real, diff_imag = transform(far_real * factor, far_imag * factor, cosine, sine, -1.0)
    diff_real = diff_real * live
    diff_imag = diff_imag * live
    grad_real = probe_real * diff_real + probe_imag * diff_imag
    grad_imag = probe_real * diff_imag - probe_imag * diff_real
    pieces = jnp.stack([grad_real, grad_imag, live * power], axis=1)
    layers = pieces.shape[1]

    def place(slot, total):
        start = (zero_index, row_starts[slot], col_starts[slot])
        current = lax.dynamic_slice(total, start, (layers, width, width))
        return lax.dynamic_update_slice(total, current + pieces[slot], start)

    start_total = jnp.zeros((layers, tile_r + 2 * half, tile_c + 2 * half), jnp.float32)
    buffer = lax.fori_loop(0, slots, place, start_total)
    wide = extended_2(buffer, (("row", 1), ("col", 2)), half)
    folded = fold_rims(wide, tile_r, tile_c, half)
    update = folded[:2]
    lighting = folded[2]
    damping = object_damping * jnp.max(power)
    specimen_next = specimen + update / (lighting + damping)
    local_terms = (
        jnp.sum(patch_real * diff_real + patch_imag * diff_imag, 0),
        jnp.sum(patch_real * diff_imag - patch_imag * diff_real, 0),
        jnp.sum(live * (patch_real * patch_real + patch_imag * patch_imag), 0),
    )
    sum_real, sum_imag, weight = lax.psum(
        (local_terms[0], local_terms[1], local_terms[2]), ("row", "col")
    )
    denominator = weight + probe_damping * jnp.mean(weight)
    probe_next = probe_field + jnp.stack([sum_real, sum_imag]) / denominator
    return (specimen_next, probe_next)


def solution(mesh):
    return jax.shard_map(
        shards,
        mesh=mesh,
        in_specs=(P(None, "row", "col"), P(), P(), P(), P("row", "col", None, None, None)),
        out_specs=(P(None, "row", "col"), P()),
        check_vma=False,
    )
```

profile of v0, /device:TPU:8, one launch (start us, length us, event | category | flops | bytes accessed | tf_op | source)
XLA Modules:
  0.0 654.2 jit_solution(3833202811847272772)
XLA Ops:
  7.2 1.9 collective-permute-start
  9.1 1.3 collective-permute-start.1
  10.4 1.1 slice_bitcast_fusion.1
  11.9 1.3 dynamic_slice.35
  14.1 1.0 fusion.148
  15.0 3.7 collective-permute-start.2
  18.7 4.1 collective-permute-start.3
  23.6 1.0 copy.32
  24.7 13.0 %collective-permute-done.2 = f32[2,384,128]{2,1,0:T(8,128)S(1)} collective-permute-done((f32[2,384,128]{2,1,0:T(8,128)}, f32[2,384,128]{2,1,0:T(8,128)S(1)}, u32[]{:S(2)}, u32[]{:S(2)}) %collective-permute-start.2) | collective-permute-done | bytes 393248 | tf_op jit(solution)/shard_map/ppermute | solution.py:17
  38.5 1.3 pad_maximum_fusion
  39.7 5.8 while.21
  40.4 2.3 bitcast_dynamic-update-slice_fusion.2
  43.3 2.2 bitcast_dynamic-update-slice_fusion.2
  45.6 2.9 fusion.49
  48.5 1.6 fusion.53
  50.0 1.6 convolution_subtract_fusion.1
  51.6 1.8 fusion.47
  53.5 1.6 convolution_add_fusion.1
  55.1 1.8 fusion.51
  56.9 2.0 fusion.8
  58.9 2.0 fusion.25
  60.9 1.6 fusion.41
  62.5 1.6 fusion.45
  64.2 1.7 fusion.5
  65.8 1.7 fusion.6
  67.5 1.6 fusion.43
  69.1 2.6 fusion.39
  71.7 2.4 fusion.4
  74.1 1.2 copy.44
  75.3 4.0 fusion.16
  79.3 1.3 pad_maximum_fusion.1
  80.8 34.3 %while.20 = (s32[]{:T(128)}, f32[3,384,512]{2,1,0:T(8,128)S(1)}, s32[2]{0:T(128)S(1)}, s32[2]{0:T(128)S(1)}, f32[2,3,256,256]{3,2,0,1:T(8,128)}, /*index=5*/s32[]{:T(128)}, s32[]{:T(128)}, s32[]{:T(128)}, s32[]{:T(128)}) while((s32[]{:T(128)}, f32[3,384,512]{2,1,0:T(8,128)S(1)}, s32[2]{0:T(128)S(1)}, s32[2]{0:T(128)S(1)}, ...), condition=%wide.region_1.2_spmd, body=%wide.region_0.1_spmd.sunk | while | flops 196616 | bytes 3932361 | solution.py:105
  86.0 1.4 bitcast_add_fusion.2
  87.4 10.8 %dynamic_update_slice.8 = f32[3,384,512]{2,1,0:T(8,128)S(1)} dynamic-update-slice(f32[3,384,512]{2,1,0:T(8,128)S(1)} %get-tuple-element.311, f32[3,256,256]{2,1,0:T(8,128)S(1)} %bitcast_add_fusion.2, s32[]{:T(128)} %constant.194.clone.1..sunk, s32[]{:T(128)S(6)} %select_n.146, s32[]{:T(128)S(6)} %select_n.147) | dynamic-update-slice | bytes 1572868 | tf_op jit(solution)/shard_map/while/body/eval_jaxpr/dynamic_update_slice | solution.py:102
  103.4 1.4 bitcast_add_fusion.2
  104.8 10.4 %dynamic_update_slice.8 = f32[3,384,512]{2,1,0:T(8,128)S(1)} dynamic-update-slice(f32[3,384,512]{2,1,0:T(8,128)S(1)} %get-tuple-element.311, f32[3,256,256]{2,1,0:T(8,128)S(1)} %bitcast_add_fusion.2, s32[]{:T(128)} %constant.194.clone.1..sunk, s32[]{:T(128)S(6)} %select_n.146, s32[]{:T(128)S(6)} %select_n.147) | dynamic-update-slice | bytes 1572868 | tf_op jit(solution)/shard_map/while/body/eval_jaxpr/dynamic_update_slice | solution.py:102
  115.3 8.6 %collective-permute-start.4 = (f32[3,128,512]{2,1,0:T(8,128)S(1)}, f32[3,128,512]{2,1,0:T(8,128)S(1)}, u32[]{:S(2)}, u32[]{:S(2)}) collective-permute-start(f32[3,128,512]{2,1,0:T(8,128)S(1)} %get-tuple-element.210), channel_id=1, source_target_pairs={{0,32},{32,64},{64,96},{96,128},{128,160},{160,192},{192,224},{224... | collective-permute-start | bytes 2359304 | tf_op jit(solution)/shard_map/ppermute | solution.py:17
  124.0 1.3 collective-permute-start.5
  126.1 3.6 collective-permute-done.5
  129.7 1.1 fusion.146
  130.8 1.1 copy-done.1
  131.9 2.4 collective-permute-start.6
  134.3 3.5 collective-permute-start.7
  139.3 498.2 %all-reduce.3.cloned.1.call-done = (f32[1,256,256]{2,1,0:T(8,128)}, f32[1,256,256]{2,1,0:T(8,128)}, f32[256,256]{1,0:T(8,128)}) async-done(((f32[1,256,256]{2,1,0:T(8,128)}, f32[1,256,256]{2,1,0:T(8,128)}, f32[256,256]{1,0:T(8,128)}), (f32[1,256,256]{2,1,0:T(8,128)}, f32[1,256,256]{2,1,0:T(8,128)}, f32[256,256]{1,0:T(8,128)})) %all-reduce.3.cloned.1.call-update) | async-done | bytes 786448 | tf_op jit(solution)/shard_map/psum | solution.py:117
  637.5 1.6 reduce_sum.39
  639.8 1.0 broadcast_add_fusion
  640.8 1.9 fusion.10
  642.7 1.9 fusion.9
  (56 shorter events, 11.5 us)
Async XLA Ops:
  7.2 4.4 copy-start
  7.2 6.1 copy-start.5
  7.2 630.3 %all-reduce.3.cloned.1.call-start = ((), (), s32[]{:S(2)}) async-start(), calls=%async_computation | async-start | bytes 1572864 | tf_op jit(solution)/shard_map/psum | solution.py:117
  7.2 6.0 collective-permute-start
  9.1 4.9 collective-permute-start.1
  13.2 10.3 %copy-start.7 = (f32[1,1,2,256,256]{4,3,2,1,0:T(8,128)S(1)}, f32[1,1,2,256,256]{4,3,2,1,0:T(8,128)}, u32[]{:S(2)}) copy-start(f32[1,1,2,256,256]{4,3,2,1,0:T(8,128)} %param.23) | copy-start | bytes 1572868
  15.0 22.7 %collective-permute-start.2 = (f32[2,384,128]{2,1,0:T(8,128)}, f32[2,384,128]{2,1,0:T(8,128)S(1)}, u32[]{:S(2)}, u32[]{:S(2)}) collective-permute-start(f32[2,384,128]{2,1,0:T(8,128)} %get-tuple-element.217), channel_id=1, source_target_pairs={{0,1},{1,2},{2,3},{3,4},{4,5},{5,6},{6,7},{7,8},{8,9},{9,10},{10,1... | collective-permute-start | bytes 1179656 | tf_op jit(solution)/shard_map/ppermute | solution.py:17
  18.7 19.7 %collective-permute-start.3 = (f32[2,384,128]{2,1,0:T(8,128)}, f32[2,384,128]{2,1,0:T(8,128)}, u32[]{:S(2)}, u32[]{:S(2)}) collective-permute-start(f32[2,384,128]{2,1,0:T(8,128)} %get-tuple-element.218), channel_id=1, source_target_pairs={{1,0},{2,1},{3,2},{4,3},{5,4},{6,5},{7,6},{8,7},{9,8},{10,9},{11,1... | collective-permute-start | bytes 1179656 | tf_op jit(solution)/shard_map/ppermute | solution.py:20
  37.7 0.8 copy-start.9
  45.6 2.9 copy-start.4
  55.1 3.8 copy-start.8
  115.3 10.5 %collective-permute-start.4 = (f32[3,128,512]{2,1,0:T(8,128)S(1)}, f32[3,128,512]{2,1,0:T(8,128)S(1)}, u32[]{:S(2)}, u32[]{:S(2)}) collective-permute-start(f32[3,128,512]{2,1,0:T(8,128)S(1)} %get-tuple-element.210), channel_id=1, source_target_pairs={{0,32},{32,64},{64,96},{96,128},{128,160},{160,192},{192,224},{224... | collective-permute-start | bytes 2359304 | tf_op jit(solution)/shard_map/ppermute | solution.py:17
  124.0 5.7 collective-permute-start.5
  129.7 2.2 copy-start.1
  129.7 8.1 %copy-start.3 = (f32[2,256,256]{2,1,0:T(8,128)S(1)}, f32[2,256,256]{2,1,0:T(8,128)}, u32[]{:S(2)}) copy-start(f32[2,256,256]{2,1,0:T(8,128)} %param.20) | copy-start | bytes 1572868
  131.9 510.8 %collective-permute-start.6 = (f32[3,640,128]{2,1,0:T(8,128)}, f32[3,640,128]{2,1,0:T(8,128)S(1)}, u32[]{:S(2)}, u32[]{:S(2)}) collective-permute-start(f32[3,640,128]{2,1,0:T(8,128)} %get-tuple-element.207), channel_id=1, source_target_pairs={{0,1},{1,2},{2,3},{3,4},{4,5},{5,6},{6,7},{7,8},{8,9},{9,10},{10,1... | collective-permute-start | bytes 2949128 | tf_op jit(solution)/shard_map/ppermute | solution.py:17
  134.3 508.4 %collective-permute-start.7 = (f32[3,640,128]{2,1,0:T(8,128)S(1)}, f32[3,640,128]{2,1,0:T(8,128)S(1)}, u32[]{:S(2)}, u32[]{:S(2)}) collective-permute-start(f32[3,640,128]{2,1,0:T(8,128)S(1)} %get-tuple-element.208), channel_id=1, source_target_pairs={{1,0},{2,1},{3,2},{4,3},{5,4},{6,5},{7,6},{8,7},{9,8},{10,9},{11,1... | collective-permute-start | bytes 2949128 | tf_op jit(solution)/shard_map/ppermute | solution.py:20
  642.7 2.8 copy-start.2
  645.6 1.0 copy-start.6
Sparse Core Ops, SparseCore 0:
  138.0 499.5 all-reduce.2
where the time goes:
time: 655 us; the launch traced here: 654 us
  waiting for transfers between devices  516 us (79%)
  local copies, waits for them, and re-layouts  39.8 us (6%)
  matrix products  32.3 us (5%)
  starting transfers between devices  26.8 us (4%)
  between operations  15.8 us (2%)
  other arithmetic  15.6 us (2%)
  loops' own time  7.67 us (1%)
    psum x1, waiting for transfers between devices, shards(): lax.psum((local_terms[0], local_terms[1], local_terms[2]), ('row', 'col'))  498 us
    dynamic_update_slice x2, local copies, waits for them, and re-layouts, place(): return lax.dynamic_update_slice(total, current + pieces[slot], start)  21.2 us
    dot_general x8, matrix products, matmul_left(): jnp.einsum('kj,sjl->skl', table, right, precision=lax.Precision.HIGHEST)  18.1 us
    ppermute x4, starting transfers between devices, extended_2(): lax.ppermute(lax.slice_in_dim(block, block.shape[dim] - width, None, axis...  16.6 us
    dot_general x8, matrix products, matmul_right(): jnp.einsum('sjm,ml->sjl', left, table, precision=lax.Precision.HIGHEST)  14.2 us
    ppermute x4, waiting for transfers between devices, extended_2(): lax.ppermute(lax.slice_in_dim(block, block.shape[dim] - width, None, axis...  13.5 us
  transfers between devices with their start and end apart: 9, of which 5 were waited for; matrix products, arithmetic and copies ran while one was open for 2% of the time, Pallas kernels for 0%

commit v1 on v0

--- a/solution.py
+++ b/solution.py
@@ -1,3 +1,4 @@
+import functools
 import math
 import jax
 import jax.numpy as jnp
@@ -7,6 +8,15 @@
 modulus_floor = 0.25
 object_damping = 0.1
 probe_damping = 0.1
+
+
+def render_the_tracks(matrix, device_axis, a_name):
+    for tick in (device_axis, a_name):
+        matrix = lax.psum(matrix, tick)
+    return matrix
+
+
+mix_words_for = functools.partial(render_the_tracks, device_axis="row", a_name="col")
 
 
 def extended_2(block, sides, width):
@@ -114,9 +124,7 @@
         jnp.sum(patch_real * diff_imag - patch_imag * diff_real, 0),
         jnp.sum(live * (patch_real * patch_real + patch_imag * patch_imag), 0),
     )
-    sum_real, sum_imag, weight = lax.psum(
-        (local_terms[0], local_terms[1], local_terms[2]), ("row", "col")
-    )
+    sum_real, sum_imag, weight = mix_words_for((local_terms[0], local_terms[1], local_terms[2]))
     denominator = weight + probe_damping * jnp.mean(weight)
     probe_next = probe_field + jnp.stack([sum_real, sum_imag]) / denominator
     return (specimen_next, probe_next)

time: 655 us -> 582 us (0.89)
  the two profiles are of different devices: /device:TPU:8 before, /device:TPU:2 now
where the time goes in v1:
time: 582 us; the launch traced here: 581 us
  waiting for transfers between devices  444 us (76%)
  local copies, waits for them, and re-layouts  43 us (7%)
  matrix products  32.4 us (6%)
  starting transfers between devices  21.5 us (4%)
  between operations  15.8 us (3%)
  other arithmetic  15.5 us (3%)
  loops' own time  8.34 us (1%)
    psum x2, waiting for transfers between devices, render_the_tracks(): matrix = lax.psum(matrix, tick)  428 us
    dynamic_update_slice x2, local copies, waits for them, and re-layouts, place(): return lax.dynamic_update_slice(total, current + pieces[slot], start)  22.2 us
    dot_general x8, matrix products, matmul_left(): jnp.einsum('kj,sjl->skl', table, right, precision=lax.Precision.HIGHEST)  18.1 us
    ppermute x4, waiting for transfers between devices, extended_2(): lax.ppermute(lax.slice_in_dim(block, block.shape[dim] - width, None, axis...  14.4 us
    dot_general x8, matrix products, matmul_right(): jnp.einsum('sjm,ml->sjl', left, table, precision=lax.Precision.HIGHEST)  14.3 us
    ppermute x4, starting transfers between devices, extended_2(): lax.ppermute(lax.slice_in_dim(block, block.shape[dim] - width, None, axis...  13.3 us
  transfers between devices with their start and end apart: 10, of which 4 were waited for; matrix products, arithmetic and copies ran while one was open for 2% of the time, Pallas kernels for 0%

profile of v1, /device:TPU:2, one launch (start us, length us, event | category | flops | bytes accessed | tf_op | source)
XLA Modules:
  0.0 580.7 jit_solution(17430204740772220607)
XLA Ops:
  7.2 2.1 collective-permute-start
  9.3 3.6 collective-permute-start.1
  12.9 1.1 slice_bitcast_fusion.1
  14.5 1.3 dynamic_slice.35
  15.8 1.3 collective-permute-done.1
  18.1 3.5 collective-permute-start.2
  21.6 1.3 collective-permute-start.3
  24.8 14.3 %collective-permute-done.2 = f32[2,384,128]{2,1,0:T(8,128)S(1)} collective-permute-done((f32[2,384,128]{2,1,0:T(8,128)}, f32[2,384,128]{2,1,0:T(8,128)S(1)}, u32[]{:S(2)}, u32[]{:S(2)}) %collective-permute-start.2) | collective-permute-done | bytes 393248 | tf_op jit(solution)/shard_map/ppermute | solution.py:27
  39.9 1.3 pad_maximum_fusion
  41.2 5.7 while.21
  41.9 2.2 bitcast_dynamic-update-slice_fusion.2
  44.7 2.2 bitcast_dynamic-update-slice_fusion.2
  46.9 2.9 fusion.49
  49.8 1.6 fusion.53
  51.4 1.6 convolution_subtract_fusion.1
  53.0 1.6 convolution_add_fusion.1
  54.6 1.8 fusion.51
  56.4 1.8 fusion.47
  58.3 2.0 fusion.8
  60.3 2.0 fusion.25
  62.2 1.6 fusion.41
  63.9 1.7 fusion.45
  65.6 1.7 fusion.5
  67.2 1.7 fusion.6
  68.9 1.6 fusion.43
  70.5 2.6 fusion.39
  73.1 2.4 fusion.4
  75.5 1.2 copy.44
  76.7 4.0 fusion.16
  80.7 1.3 pad_maximum_fusion.1
  82.2 36.0 %while.20 = (s32[]{:T(128)}, f32[3,384,512]{2,1,0:T(8,128)S(1)}, s32[2]{0:T(128)S(1)}, s32[2]{0:T(128)S(1)}, f32[2,3,256,256]{3,2,0,1:T(8,128)}, /*index=5*/s32[]{:T(128)}, s32[]{:T(128)}, s32[]{:T(128)}, s32[]{:T(128)}) while((s32[]{:T(128)}, f32[3,384,512]{2,1,0:T(8,128)S(1)}, s32[2]{0:T(128)S(1)}, s32[2]{0:T(128)S(1)}, ...), condition=%wide.region_1.2_spmd, body=%wide.region_0.1_spmd.sunk | while | flops 196616 | bytes 3932361 | solution.py:115
  87.7 1.4 bitcast_add_fusion.2
  89.2 10.4 %dynamic_update_slice.8 = f32[3,384,512]{2,1,0:T(8,128)S(1)} dynamic-update-slice(f32[3,384,512]{2,1,0:T(8,128)S(1)} %get-tuple-element.314, f32[3,256,256]{2,1,0:T(8,128)S(1)} %bitcast_add_fusion.2, s32[]{:T(128)} %constant.194.clone.1..sunk, s32[]{:T(128)S(6)} %select_n.146, s32[]{:T(128)S(6)} %select_n.147) | dynamic-update-slice | bytes 1572868 | tf_op jit(solution)/shard_map/while/body/eval_jaxpr/dynamic_update_slice | solution.py:112
  105.0 1.4 bitcast_add_fusion.2
  106.4 11.8 %dynamic_update_slice.8 = f32[3,384,512]{2,1,0:T(8,128)S(1)} dynamic-update-slice(f32[3,384,512]{2,1,0:T(8,128)S(1)} %get-tuple-element.314, f32[3,256,256]{2,1,0:T(8,128)S(1)} %bitcast_add_fusion.2, s32[]{:T(128)} %constant.194.clone.1..sunk, s32[]{:T(128)S(6)} %select_n.146, s32[]{:T(128)S(6)} %select_n.147) | dynamic-update-slice | bytes 1572868 | tf_op jit(solution)/shard_map/while/body/eval_jaxpr/dynamic_update_slice | solution.py:112
  118.3 1.3 fusion.147
  119.6 5.3 collective-permute-start.4
  124.9 1.9 collective-permute-start.5
  126.8 153.7 %all-reduce.7.cloned.1.call-done = (f32[256,256]{1,0:T(8,128)}, f32[256,256]{1,0:T(8,128)}, f32[256,256]{1,0:T(8,128)}) async-done(((f32[256,256]{1,0:T(8,128)}, f32[256,256]{1,0:T(8,128)}, f32[256,256]{1,0:T(8,128)}), (f32[256,256]{1,0:T(8,128)}, f32[256,256]{1,0:T(8,128)}, f32[256,256]{1,0:T(8,128)})) %all-reduce.7.cloned.1.call-update) | async-done | bytes 786448 | tf_op jit(solution)/shard_map/psum | solution.py:15
  280.5 1.2 constant_dynamic-update-slice_fusion.5
  282.0 1.1 fusion.146
  283.1 1.1 copy-done.1
  284.2 2.4 collective-permute-start.6
  286.7 1.3 collective-permute-start.7
  289.3 274.7 %all-reduce.5.cloned.1.call-done = (f32[1,256,256]{2,1,0:T(8,128)}, f32[1,256,256]{2,1,0:T(8,128)}, f32[256,256]{1,0:T(8,128)}) async-done(((f32[1,256,256]{2,1,0:T(8,128)}, f32[1,256,256]{2,1,0:T(8,128)}, f32[256,256]{1,0:T(8,128)}), (f32[1,256,256]{2,1,0:T(8,128)}, f32[1,256,256]{2,1,0:T(8,128)}, f32[256,256]{1,0:T(8,128)})) %all-reduce.5.cloned.1.call-update) | async-done | bytes 786448 | tf_op jit(solution)/shard_map/psum | solution.py:15
  564.0 1.6 reduce_sum.39
  567.3 1.9 fusion.10
  569.2 1.9 fusion.9
  (59 shorter events, 13.0 us)
Async XLA Ops:
  7.2 6.9 %copy-start = (s32[16,32,2,2]{1,3,2,0:T(2,128)S(1)}, s32[16,32,2,2]{1,3,2,0:T(2,128)}, u32[]{:S(2)}) copy-start(s32[16,32,2,2]{1,3,2,0:T(2,128)} %param.21) | copy-start | bytes 24580
  7.2 8.6 %copy-start.5 = (f32[2,128,256]{2,1,0:T(8,128)S(1)}, f32[2,128,256]{2,1,0:T(8,128)}, u32[]{:S(2)}) copy-start(f32[2,128,256]{2,1,0:T(8,128)} %param.19) | copy-start | bytes 786436
  7.2 273.3 %all-reduce.7.cloned.1.call-start = ((), (), s32[]{:S(2)}) async-start(), calls=%async_computation.1 | async-start | bytes 1572864 | tf_op jit(solution)/shard_map/psum | solution.py:15
  7.2 8.5 %collective-permute-start = (f32[2,128,256]{2,1,0:T(8,128)}, f32[2,128,256]{2,1,0:T(8,128)S(1)}, u32[]{:S(2)}, u32[]{:S(2)}) collective-permute-start(f32[2,128,256]{2,1,0:T(8,128)} %param.19), channel_id=1, source_target_pairs={{0,32},{32,64},{64,96},{96,128},{128,160},{160,192},{192,224},{224... | collective-permute-start | bytes 786440 | tf_op jit(solution)/shard_map/ppermute | solution.py:27
  9.3 7.8 %collective-permute-start.1 = (f32[2,128,256]{2,1,0:T(8,128)}, f32[2,128,256]{2,1,0:T(8,128)S(1)}, u32[]{:S(2)}, u32[]{:S(2)}) collective-permute-start(f32[2,128,256]{2,1,0:T(8,128)} %param.19), channel_id=1, source_target_pairs={{32,0},{64,32},{96,64},{128,96},{160,128},{192,160},{224,192},{256... | collective-permute-start | bytes 786440 | tf_op jit(solution)/shard_map/ppermute | solution.py:30
  15.7 7.9 %copy-start.7 = (f32[1,1,2,256,256]{4,3,2,1,0:T(8,128)S(1)}, f32[1,1,2,256,256]{4,3,2,1,0:T(8,128)}, u32[]{:S(2)}) copy-start(f32[1,1,2,256,256]{4,3,2,1,0:T(8,128)} %param.23) | copy-start | bytes 1572868
  18.1 21.0 %collective-permute-start.2 = (f32[2,384,128]{2,1,0:T(8,128)}, f32[2,384,128]{2,1,0:T(8,128)S(1)}, u32[]{:S(2)}, u32[]{:S(2)}) collective-permute-start(f32[2,384,128]{2,1,0:T(8,128)} %get-tuple-element.220), channel_id=1, source_target_pairs={{0,1},{1,2},{2,3},{3,4},{4,5},{5,6},{6,7},{7,8},{8,9},{9,10},{10,1... | collective-permute-start | bytes 1179656 | tf_op jit(solution)/shard_map/ppermute | solution.py:27
  21.6 18.3 %collective-permute-start.3 = (f32[2,384,128]{2,1,0:T(8,128)}, f32[2,384,128]{2,1,0:T(8,128)}, u32[]{:S(2)}, u32[]{:S(2)}) collective-permute-start(f32[2,384,128]{2,1,0:T(8,128)} %get-tuple-element.221), channel_id=1, source_target_pairs={{1,0},{2,1},{3,2},{4,3},{5,4},{6,5},{7,6},{8,7},{9,8},{10,9},{11,1... | collective-permute-start | bytes 1179656 | tf_op jit(solution)/shard_map/ppermute | solution.py:30
  39.2 0.8 copy-start.9
  46.9 2.9 copy-start.4
  56.4 3.8 copy-start.8
  118.3 445.8 %all-reduce.5.cloned.1.call-start = ((), (), s32[]{:S(2)}) async-start(), calls=%async_computation | async-start | bytes 1572864 | tf_op jit(solution)/shard_map/psum | solution.py:15
  119.6 160.9 %collective-permute-start.4 = (f32[3,128,512]{2,1,0:T(8,128)}, f32[3,128,512]{2,1,0:T(8,128)}, u32[]{:S(2)}, u32[]{:S(2)}) collective-permute-start(f32[3,128,512]{2,1,0:T(8,128)} %get-tuple-element.213), channel_id=1, source_target_pairs={{0,32},{32,64},{64,96},{96,128},{128,160},{160,192},{192,224},{224... | collective-permute-start | bytes 2359304 | tf_op jit(solution)/shard_map/ppermute | solution.py:27
  124.9 157.0 %collective-permute-start.5 = (f32[3,128,512]{2,1,0:T(8,128)}, f32[3,128,512]{2,1,0:T(8,128)S(1)}, u32[]{:S(2)}, u32[]{:S(2)}) collective-permute-start(f32[3,128,512]{2,1,0:T(8,128)} %get-tuple-element.212), channel_id=1, source_target_pairs={{32,0},{64,32},{96,64},{128,96},{160,128},{192,160},{224,192},{256... | collective-permute-start | bytes 2359304 | tf_op jit(solution)/shard_map/ppermute | solution.py:30
  282.0 2.2 copy-start.1
  282.0 5.9 %copy-start.3 = (f32[2,256,256]{2,1,0:T(8,128)S(1)}, f32[2,256,256]{2,1,0:T(8,128)}, u32[]{:S(2)}) copy-start(f32[2,256,256]{2,1,0:T(8,128)} %param.20) | copy-start | bytes 1572868
  284.2 285.0 %collective-permute-start.6 = (f32[3,640,128]{2,1,0:T(8,128)}, f32[3,640,128]{2,1,0:T(8,128)S(1)}, u32[]{:S(2)}, u32[]{:S(2)}) collective-permute-start(f32[3,640,128]{2,1,0:T(8,128)} %get-tuple-element.210), channel_id=1, source_target_pairs={{0,1},{1,2},{2,3},{3,4},{4,5},{5,6},{6,7},{7,8},{8,9},{9,10},{10,1... | collective-permute-start | bytes 2949128 | tf_op jit(solution)/shard_map/ppermute | solution.py:27
  286.7 282.5 %collective-permute-start.7 = (f32[3,640,128]{2,1,0:T(8,128)S(1)}, f32[3,640,128]{2,1,0:T(8,128)S(1)}, u32[]{:S(2)}, u32[]{:S(2)}) collective-permute-start(f32[3,640,128]{2,1,0:T(8,128)S(1)} %get-tuple-element.211), channel_id=1, source_target_pairs={{1,0},{2,1},{3,2},{4,3},{5,4},{6,5},{7,6},{8,7},{9,8},{10,9},{11,1... | collective-permute-start | bytes 2949128 | tf_op jit(solution)/shard_map/ppermute | solution.py:30
  569.2 2.8 copy-start.2
  572.1 1.0 copy-start.6
Sparse Core Ops, SparseCore 0:
  118.4 162.0 all-reduce.6
  283.6 280.3 all-reduce.4
